TPU v7x, 32 devices: a whole 2x2x4 slice. The times are simulated.
32 devices in a mesh: dp: 8 (over y, x, core), mp: 4 (over z).
Axes of the slice: x: 2, y: 2, z: 4, core: 2. Of those that a mesh axis runs over, the one named last changes fastest.
Arguments:
- query_new: bfloat16 [32, 4096], P(('dp', 'mp')), parts along dimension 0, may hold values from -140 to 140
- key_new: bfloat16 [32, 1024], P(('dp', 'mp')), parts along dimension 0, may hold values from -5 to 5
- value_new: bfloat16 [32, 1024], P(('dp', 'mp')), parts along dimension 0, may hold values from -5 to 5
- prefix_keys: bfloat16 [4096, 1024], P(('dp', 'mp')), parts along dimension 0, may hold values from -5 to 5
- prefix_values: bfloat16 [4096, 1024], P(('dp', 'mp')), parts along dimension 0, may hold values from -5 to 5
- sample_suffix_keys: bfloat16 [32, 64, 1024], P(('dp', 'mp')), parts along dimension 0, may hold values from -5 to 5
- sample_suffix_values: bfloat16 [32, 64, 1024], P(('dp', 'mp')), parts along dimension 0, may hold values from -5 to 5
- prefix_len: int32 [8], P('dp'), parts along dimension 0, may hold values from 128 to 512
- suffix_len: int32 [32], P(('dp', 'mp')), parts along dimension 0, may hold values from 1 to 64, as said below
- residual: bfloat16 [32, 8192], P(('dp', 'mp')), parts along dimension 0, may hold values from -3 to 3
- out_weight: bfloat16 [4096, 8192], P('mp'), may hold values from -0.1875 to 0.1875
- norm_gain: bfloat16 [8192], replicated, may hold values from 0.5 to 1.5
Outputs:
- hidden: bfloat16 [32, 8192], P(('dp', 'mp')), parts along dimension 0
- normed: bfloat16 [32, 8192], P(('dp', 'mp')), parts along dimension 0
There are 8 independent parts, one for each index of `dp`. A program takes and returns all parts, laid end to end along the dimension named above; an argument that names none is the same for every part. Nothing has to cross between parts.
Inputs may be any that keep to these rules, and one draw needn't show every extreme that they name: `suffix_len`: some sample has exactly 64 cached generated tokens.
All inputs are finite; a program needn't handle non-finite values.
Results may differ from a plain program's by a relative error of at most 0.0085.
Values may be sent and summed in bfloat16 or wider, within the bound.
A program may use at most 64 MiB of HBM per device.

v0:
```python
import jax
import jax.numpy as jnp
from jax import lax
from jax.sharding import PartitionSpec as P

HEAD_SIZE = 128
KEY_VALUE_HEADS = 8
HQ = 32


def local(
    query_new,
    key_new,
    value_new,
    prefix_keys,
    prefix_values,
    sample_suffix_keys,
    sample_suffix_values,
    prefix_len,
    suffix_len,
    residual,
    out_weight,
    norm_gain,
):
    count_mp = lax.axis_size("mp")
    place = lax.axis_index("mp")
    samples_per_part = query_new.shape[0]
    batch = samples_per_part * count_mp
    heads_dev = out_weight.shape[0] // HEAD_SIZE
    group = HQ // KEY_VALUE_HEADS
    pre_dev = prefix_keys.shape[0]
    suffix_result = sample_suffix_keys.shape[1]
    score_scale = HEAD_SIZE ** (-0.5)
    first_row = place * samples_per_part
    queries = lax.all_gather(query_new, "mp", axis=0, tiled=True)
    query_all = queries.reshape(batch, KEY_VALUE_HEADS, group, HEAD_SIZE)
    pkeys = prefix_keys.reshape(pre_dev, KEY_VALUE_HEADS, HEAD_SIZE)
    prefix_value_rows = prefix_values.reshape(pre_dev, KEY_VALUE_HEADS, HEAD_SIZE)
    s_pre = (
        jnp.einsum("bkgd,pkd->bkgp", query_all, pkeys, preferred_element_type=jnp.float32)
        * score_scale
    )
    positions = place * pre_dev + lax.iota(jnp.int32, pre_dev)
    pvalid = (positions < prefix_len[0])[None, None, None, :]
    s_pre = jnp.where(pvalid, s_pre, -jnp.inf)
    query_sample_rows = query_new.reshape(samples_per_part, KEY_VALUE_HEADS, group, HEAD_SIZE)
    suffix_key_rows = sample_suffix_keys.reshape(
        samples_per_part, suffix_result, KEY_VALUE_HEADS, HEAD_SIZE
    )
    suffix_value_rows = sample_suffix_values.reshape(
        samples_per_part, suffix_result, KEY_VALUE_HEADS, HEAD_SIZE
    )
    nvals = value_new.reshape(samples_per_part, KEY_VALUE_HEADS, HEAD_SIZE)
    suffix_score_rows = (
        jnp.einsum(
            "cqxt,caqt->cqxa",
            query_sample_rows,
            suffix_key_rows,
            preferred_element_type=jnp.float32,
        )
        * score_scale
    )
    svalid = (lax.iota(jnp.int32, suffix_result)[None, :] < suffix_len[:, None])[:, None, None, :]
    suffix_score_rows = jnp.where(svalid, suffix_score_rows, -jnp.inf)
    fresh_score_rows = (
        jnp.einsum(
            "exio,exo->exi",
            query_sample_rows,
            key_new.reshape(samples_per_part, KEY_VALUE_HEADS, HEAD_SIZE),
            preferred_element_type=jnp.float32,
        )
        * score_scale
    )
    top_pre = jnp.maximum(jnp.max(s_pre, -1), -1e30)
    own_top = lax.dynamic_slice_in_dim(top_pre, first_row, samples_per_part, 0)
    own_top = jnp.maximum(jnp.maximum(own_top, jnp.max(suffix_score_rows, -1)), fresh_score_rows)
    local_top = lax.dynamic_update_slice_in_dim(top_pre, own_top, first_row, 0)
    top_own = lax.dynamic_slice_in_dim(local_top, first_row, samples_per_part, 0)
    w_pre = jnp.where(pvalid, jnp.exp(s_pre - local_top[..., None]), 0.0)
    total = jnp.sum(w_pre, -1)
    summed_rows = jnp.einsum(
        "wnso,onr->wnsr",
        w_pre.astype(jnp.bfloat16),
        prefix_value_rows,
        preferred_element_type=jnp.float32,
    )
    suffix_weight_rows = jnp.where(svalid, jnp.exp(suffix_score_rows - top_own[..., None]), 0.0)
    w_new = jnp.exp(fresh_score_rows - top_own)
    own_total = jnp.sum(suffix_weight_rows, -1) + w_new
    own_sum = jnp.einsum(
        "cjax,cxjq->cjaq",
        suffix_weight_rows.astype(jnp.bfloat16),
        suffix_value_rows,
        preferred_element_type=jnp.float32,
    )
    own_sum = (
        own_sum
        + w_new.astype(jnp.bfloat16).astype(jnp.float32)[..., None]
        * nvals.astype(jnp.float32)[:, :, None, :]
    )
    total = lax.dynamic_update_slice_in_dim(
        total,
        lax.dynamic_slice_in_dim(total, first_row, samples_per_part, 0) + own_total,
        first_row,
        0,
    )
    summed_rows = lax.dynamic_update_slice_in_dim(
        summed_rows,
        lax.dynamic_slice_in_dim(summed_rows, first_row, samples_per_part, 0) + own_sum,
        first_row,
        0,
    )
    top_flat = local_top.reshape(batch, HQ)
    total_flat = total.reshape(batch, HQ)
    summed_flat = summed_rows.reshape(batch, HQ, HEAD_SIZE)
    parts = (
        lax.all_to_all(top_flat[None], "mp", split_axis=2, concat_axis=0, tiled=True),
        lax.all_to_all(total_flat[None], "mp", split_axis=2, concat_axis=0, tiled=True),
        lax.all_to_all(summed_flat[None], "mp", split_axis=2, concat_axis=0, tiled=True),
    )
    best = jnp.max(parts[0], axis=0)
    factor = jnp.exp(parts[0] - best[None])
    whole_total = jnp.sum(factor * parts[1], axis=0)
    whole_summed = jnp.sum(factor[..., None] * parts[2], axis=0)
    items = parts[0].shape[1]
    attn = (
        (whole_summed / whole_total[..., None])
        .astype(jnp.bfloat16)
        .reshape(items, heads_dev * HEAD_SIZE)
    )
    proj = lax.psum_scatter(
        jnp.dot(attn, out_weight, preferred_element_type=jnp.float32),
        "mp",
        scatter_dimension=0,
        tiled=True,
    )
    stream = residual.astype(jnp.float32) + proj
    hidden = stream.astype(jnp.bfloat16)
    meansq = jnp.mean(stream * stream, axis=-1, keepdims=True)
    normed = (stream * lax.rsqrt(meansq + 1e-05) * norm_gain.astype(jnp.float32)[None, :]).astype(
        jnp.bfloat16
    )
    return (hidden, normed)


def solution(mesh):
    placed = (
        P(("dp", "mp"), None),
        P(("dp", "mp"), None),
        P(("dp", "mp"), None),
        P(("dp", "mp"), None),
        P(("dp", "mp"), None),
        P(("dp", "mp"), None, None),
        P(("dp", "mp"), None, None),
        P("dp"),
        P(("dp", "mp")),
        P(("dp", "mp"), None),
        P("mp", None),
        P(),
    )
    return jax.shard_map(
        local,
        mesh=mesh,
        in_specs=placed,
        out_specs=(P(("dp", "mp"), None), P(("dp", "mp"), None)),
        check_vma=False,
    )
```

profile of v0, /device:TPU:0, one launch (start us, length us, event | category | flops | bytes accessed | tf_op | source)
XLA Modules:
  0.0 110.2 jit_solution(15643182920238004057)
XLA Ops:
  7.2 0.0 copy-start
  7.2 0.0 copy-start.3
  7.2 0.0 copy-start.2
  7.2 0.0 copy-start.1
  7.9 1.0 copy.106
  8.9 15.1 %all-gather = bf16[4,1,4096]{2,1,0:T(2,128)(2,1)S(1)} all-gather(bf16[1,1,4096]{2,1,0:T(2,128)(2,1)} %bitcast.113), channel_id=1, replica_groups=mesh['dp'=8,'mp'=4] {'mp'}, dimensions={0}, use_global_device_ids=true | all-gather | bytes 40960 | tf_op jit(solution)/shard_map/all_gather | solution.py:35
  24.0 0.8 reduce.7
  24.8 0.2 reduce.6
  25.0 0.3 fusion.39
  25.4 0.1 copy.68
  26.2 0.9 copy.107
  27.1 0.2 fusion.40
  27.3 0.1 copy.70
  27.4 0.0 copy-done
  27.4 0.1 fusion.31
  27.6 0.1 copy.93
  27.7 0.1 copy.76
  27.8 0.2 fusion.12
  28.0 0.1 copy.105
  28.1 0.1 copy.78
  28.2 0.2 fusion.19
  28.3 0.1 copy.85
  28.4 0.1 copy.86
  28.6 0.7 copy.101
  29.3 4.7 %all-to-all-start.2 = ((f32[1,4,32]{1,0,2:T(1,128)}), f32[1,4,32]{1,0,2:T(1,128)S(1)}, u32[]{:S(2)}, u32[]{:S(2)}) async-start(f32[1,4,32]{1,0,2:T(1,128)} %bitcast.25), calls=%async_computation.2 | async-start | bytes 32768 | tf_op jit(solution)/shard_map/all_to_all | solution.py:118
  34.0 1.0 copy.108
  35.0 0.3 fusion.6
  35.3 0.7 copy.97
  36.0 0.1 copy.80
  36.1 0.9 copy.109
  37.0 0.7 convert_element_type.50
  37.7 1.9 %all-to-all-done.2 = f32[1,4,32]{1,0,2:T(1,128)S(1)} async-done(((f32[1,4,32]{1,0,2:T(1,128)}), f32[1,4,32]{1,0,2:T(1,128)S(1)}, u32[]{:S(2)}, u32[]{:S(2)}) %all-to-all-start.2) | async-done | bytes 544 | tf_op jit(solution)/shard_map/all_to_all | solution.py:118
  39.7 3.3 %all-to-all-start = ((f32[1,4,32]{1,0,2:T(1,128)}), f32[1,4,32]{1,0,2:T(1,128)S(1)}, u32[]{:S(2)}, u32[]{:S(2)}) async-start(f32[1,4,32]{1,0,2:T(1,128)} %bitcast.9), calls=%async_computation | async-start | bytes 32768 | tf_op jit(solution)/shard_map/all_to_all | solution.py:117
  42.9 0.2 fusion.4
  43.2 0.7 copy.82
  43.8 0.1 copy.102
  43.9 4.6 %all-to-all-done = f32[1,4,32]{1,0,2:T(1,128)S(1)} async-done(((f32[1,4,32]{1,0,2:T(1,128)}), f32[1,4,32]{1,0,2:T(1,128)S(1)}, u32[]{:S(2)}, u32[]{:S(2)}) %all-to-all-start) | async-done | bytes 544 | tf_op jit(solution)/shard_map/all_to_all | solution.py:117
  48.5 3.3 %all-to-all-start.1 = ((f32[1,4,32,128]{3,1,0,2:T(4,128)}), f32[1,4,32,128]{3,1,0,2:T(4,128)S(1)}, u32[]{:S(2)}, u32[]{:S(2)}) async-start(f32[1,4,32,128]{3,1,0,2:T(4,128)} %copy.82), calls=%async_computation.1 | async-start | bytes 131072 | tf_op jit(solution)/shard_map/all_to_all | solution.py:119
  51.8 0.0 all-reduce.3.cloned.1.call-start
  51.8 0.1 copy.98
  52.0 5.5 %all-to-all-done.1 = f32[1,4,32,128]{3,1,0,2:T(4,128)S(1)} async-done(((f32[1,4,32,128]{3,1,0,2:T(4,128)}), f32[1,4,32,128]{3,1,0,2:T(4,128)S(1)}, u32[]{:S(2)}, u32[]{:S(2)}) %all-to-all-start.1) | async-done | bytes 65568 | tf_op jit(solution)/shard_map/all_to_all | solution.py:119
  57.5 0.1 fusion.11
  57.6 0.1 fusion.29
  57.7 8.7 %fusion.22 = f32[4,8192]{1,0:T(4,128)} fusion(bf16[1024,8192]{1,0:T(8,128)(2,1)} %param.22, bf16[1,4,8,128]{3,2,1,0:T(8,128)(2,1)S(1)} %fusion.29), kind=kOutput, calls=%fused_computation.30 | convolution fusion | flops 67108864 | bytes 16916480 | tf_op jit(solution)/shard_map/dot_general | solution.py:132
  66.4 0.0 all-reduce.3.cloned.1.call-update
  66.4 0.0 copy-done.2
  66.4 0.0 copy-done.3
  66.4 0.6 dynamic-slice.4
  67.0 32.7 %all-reduce.3.cloned.1.call-done = f32[4,8192]{1,0:T(4,128)} async-done(((f32[4,8192]{1,0:T(4,128)}), f32[4,8192]{1,0:T(4,128)}) %all-reduce.3.cloned.1.call-update) | async-done | bytes 131088
  99.8 0.0 copy-done.1
  99.8 2.2 %multiply_reduce_fusion = (f32[]{:T(128)}, f32[1,8192]{1,0:T(1,128)S(1)}) fusion(f32[4,8192]{1,0:T(4,128)} %all-reduce.3.cloned.1.call-done, u32[]{:T(128)} %bitcast.33, bf16[1,8192]{1,0:T(2,128)(2,1)S(1)} %copy-done.1), kind=kLoop, calls=%fused_computation.22 | loop fusion | flops 32767 | bytes 81928 | tf_op jit(solution)/shard_map/reduce_sum | solution.py:139
  102.7 0.7 multiply_convert_fusion
  (15 shorter events, 0.2 us)
Async XLA Ops:
  7.2 20.2 %copy-start = (bf16[1,1024]{1,0:T(2,128)(2,1)S(1)}, bf16[1,1024]{1,0:T(2,128)(2,1)}, u32[]{:S(2)}) copy-start(bf16[1,1024]{1,0:T(2,128)(2,1)} %param.13) | copy-start | bytes 6148
  7.2 59.2 %copy-start.3 = (u32[32]{0:T(128)S(1)}, u32[32]{0:T(128)}, u32[]{:S(2)}) copy-start(u32[32]{0:T(128)} %constant.37) | copy-start | bytes 388
  7.2 59.2 %copy-start.2 = (bf16[8192]{0:T(1024)(128)(2,1)S(1)}, bf16[8192]{0:T(1024)(128)(2,1)}, u32[]{:S(2)}) copy-start(bf16[8192]{0:T(1024)(128)(2,1)} %param.23) | copy-start | bytes 49156
  7.2 92.6 %copy-start.1 = (bf16[1,8192]{1,0:T(2,128)(2,1)S(1)}, bf16[1,8192]{1,0:T(2,128)(2,1)}, u32[]{:S(2)}) copy-start(bf16[1,8192]{1,0:T(2,128)(2,1)} %param.21) | copy-start | bytes 49156
  29.3 10.3 %all-to-all-start.2 = ((f32[1,4,32]{1,0,2:T(1,128)}), f32[1,4,32]{1,0,2:T(1,128)S(1)}, u32[]{:S(2)}, u32[]{:S(2)}) async-start(f32[1,4,32]{1,0,2:T(1,128)} %bitcast.25), calls=%async_computation.2 | async-start | bytes 32768 | tf_op jit(solution)/shard_map/all_to_all | solution.py:118
  39.7 8.8 %all-to-all-start = ((f32[1,4,32]{1,0,2:T(1,128)}), f32[1,4,32]{1,0,2:T(1,128)S(1)}, u32[]{:S(2)}, u32[]{:S(2)}) async-start(f32[1,4,32]{1,0,2:T(1,128)} %bitcast.9), calls=%async_computation | async-start | bytes 32768 | tf_op jit(solution)/shard_map/all_to_all | solution.py:117
  48.5 9.0 %all-to-all-start.1 = ((f32[1,4,32,128]{3,1,0,2:T(4,128)}), f32[1,4,32,128]{3,1,0,2:T(4,128)S(1)}, u32[]{:S(2)}, u32[]{:S(2)}) async-start(f32[1,4,32,128]{3,1,0,2:T(4,128)} %copy.82), calls=%async_computation.1 | async-start | bytes 131072 | tf_op jit(solution)/shard_map/all_to_all | solution.py:119
  51.8 48.0 %all-reduce.3.cloned.1.call-start = ((), (), s32[]{:S(2)}) async-start(), calls=%async_computation.3 | async-start | bytes 262144
Sparse Core Ops, SparseCore 0:
  66.5 33.1 all-reduce.2
where the time goes:
time: 111 us; the launch traced here: 110 us
  waiting for transfers between devices  44.8 us (40%)
  between operations  16.2 us (15%)
  blocking collectives  15.1 us (14%)
  starting transfers between devices  11.3 us (10%)
  matrix products  9.91 us (9%)
  local copies, waits for them, and re-layouts  7.66 us (7%)
  other arithmetic  5.2 us (5%)
    unnamed x2, waiting for transfers between devices  32.7 us
    all_gather x1, blocking collectives, local(): queries = lax.all_gather(query_new, 'mp', axis=0, tiled=True)  15.1 us
    dot_general x1, matrix products, local(): jnp.dot(attn, out_weight, preferred_element_type=jnp.float32)  8.71 us
    all_to_all x1, waiting for transfers between devices, local(): lax.all_to_all(summed_flat[None], 'mp', split_axis=2, concat_axis=0, tile...  5.51 us
    all_to_all x1, starting transfers between devices, local(): lax.all_to_all(total_flat[None], 'mp', split_axis=2, concat_axis=0, tiled...  4.74 us
    all_to_all x1, waiting for transfers between devices, local(): lax.all_to_all(top_flat[None], 'mp', split_axis=2, concat_axis=0, tiled=T...  4.56 us
    unnamed x15, local copies, waits for them, and re-layouts  4.53 us
    all_to_all x1, starting transfers between devices, local(): lax.all_to_all(summed_flat[None], 'mp', split_axis=2, concat_axis=0, tile...  3.28 us
  transfers between devices with their start and end apart: 4, of which 4 were waited for; matrix products, arithmetic and copies ran while one was open for 5% of the time, Pallas kernels for 0%

commit v1 on v0

--- a/solution.py
+++ b/solution.py
@@ -113,8 +113,17 @@
     top_flat = local_top.reshape(batch, HQ)
     total_flat = total.reshape(batch, HQ)
     summed_flat = summed_rows.reshape(batch, HQ, HEAD_SIZE)
+    _group_tables = lambda inner_x: jnp.concatenate(
+        lax.all_to_all(
+            jnp.stack(jnp.split(inner_x, lax.axis_size("mp"), axis=2)),
+            axis_name="mp",
+            split_axis=0,
+            concat_axis=0,
+        ),
+        axis=0,
+    )
     parts = (
-        lax.all_to_all(top_flat[None], "mp", split_axis=2, concat_axis=0, tiled=True),
+        _group_tables(top_flat[None]),
         lax.all_to_all(total_flat[None], "mp", split_axis=2, concat_axis=0, tiled=True),
         lax.all_to_all(summed_flat[None], "mp", split_axis=2, concat_axis=0, tiled=True),
     )

time: 111 us -> 111 us (level)
  no operation moved by 1% of the time
where the time goes in v1:
time: 111 us; the launch traced here: 110 us
  waiting for transfers between devices  44.7 us (40%)
  between operations  16.2 us (15%)
  blocking collectives  15.1 us (14%)
  starting transfers between devices  11.4 us (10%)
  matrix products  9.9 us (9%)
  local copies, waits for them, and re-layouts  7.11 us (6%)
  other arithmetic  5.8 us (5%)
    unnamed x2, waiting for transfers between devices  32.7 us
    all_gather x1, blocking collectives, local(): queries = lax.all_gather(query_new, 'mp', axis=0, tiled=True)  15.1 us
    dot_general x1, matrix products, local(): jnp.dot(attn, out_weight, preferred_element_type=jnp.float32)  8.71 us
    all_to_all x1, waiting for transfers between devices, local(): lax.all_to_all(summed_flat[None], 'mp', split_axis=2, concat_axis=0, tile...  5.61 us
    all_to_all x1, starting transfers between devices, local(): lax.all_to_all(total_flat[None], 'mp', split_axis=2, concat_axis=0, tiled...  4.74 us
    all_to_all x1, waiting for transfers between devices, local(): lax.all_to_all(jnp.stack(jnp.split(inner_x, lax.axis_size('mp'), axis=2))...  4.58 us
    unnamed x15, local copies, waits for them, and re-layouts  4.53 us
    all_to_all x1, starting transfers between devices, local(): lax.all_to_all(jnp.stack(jnp.split(inner_x, lax.axis_size('mp'), axis=2))...  3.32 us
  transfers between devices with their start and end apart: 4, of which 4 were waited for; matrix products, arithmetic and copies ran while one was open for 5% of the time, Pallas kernels for 0%

profile of v1, /device:TPU:0, one launch (start us, length us, event | category | flops | bytes accessed | tf_op | source)
XLA Modules:
  0.0 110.3 jit_solution(16687915880090200002)
XLA Ops:
  7.2 0.0 copy-start
  7.2 0.0 copy-start.3
  7.2 0.0 copy-start.2
  7.2 0.0 copy-start.1
  7.9 1.0 copy.95
  8.9 15.1 %all-gather = bf16[4,1,4096]{2,1,0:T(2,128)(2,1)S(1)} all-gather(bf16[1,1,4096]{2,1,0:T(2,128)(2,1)} %bitcast.116), channel_id=1, replica_groups=mesh['dp'=8,'mp'=4] {'mp'}, dimensions={0}, use_global_device_ids=true | all-gather | bytes 40960 | tf_op jit(solution)/shard_map/all_gather | solution.py:35
  24.0 0.8 reduce.7
  24.8 0.2 reduce.6
  25.0 0.3 fusion.39
  25.4 0.1 copy.63
  26.2 0.9 copy.96
  27.1 0.2 fusion.40
  27.3 0.1 copy.65
  27.4 0.0 copy-done
  27.4 0.1 fusion.31
  27.6 0.1 copy.85
  27.7 0.1 copy.68
  27.8 0.2 fusion.12
  28.0 0.1 copy.94
  28.1 0.1 copy.70
  28.2 0.2 fusion.19
  28.3 0.1 copy.77
  28.4 0.1 copy.78
  28.6 0.7 copy.91
  29.3 4.7 %all-to-all-start.2 = ((f32[1,4,32]{1,0,2:T(1,128)}), f32[1,4,32]{1,0,2:T(1,128)S(1)}, u32[]{:S(2)}, u32[]{:S(2)}) async-start(f32[1,4,32]{1,0,2:T(1,128)} %bitcast.26), calls=%async_computation.2 | async-start | bytes 32768 | tf_op jit(solution)/shard_map/all_to_all | solution.py:127
  34.0 0.1 copy.66
  34.1 0.1 broadcast_in_dim_reshape.9
  34.2 0.1 slice_bitcast_fusion.3
  34.3 1.0 copy.97
  35.3 0.3 fusion.6
  35.6 0.6 pad_maximum_fusion
  36.2 0.1 copy.72
  36.3 0.9 copy.98
  37.2 0.7 convert_element_type.50
  37.9 1.8 %all-to-all-done.2 = f32[1,4,32]{1,0,2:T(1,128)S(1)} async-done(((f32[1,4,32]{1,0,2:T(1,128)}), f32[1,4,32]{1,0,2:T(1,128)S(1)}, u32[]{:S(2)}, u32[]{:S(2)}) %all-to-all-start.2) | async-done | bytes 544 | tf_op jit(solution)/shard_map/all_to_all | solution.py:127
  39.7 3.3 %all-to-all-start = ((f32[4,1,4,8]{3,2,1,0:T(4,128)}), f32[4,1,4,8]{3,2,1,0:T(4,128)S(1)}, u32[]{:S(2)}, u32[]{:S(2)}) async-start(f32[4,1,4,8]{3,2,1,0:T(4,128)} %pad_maximum_fusion), calls=%async_computation | async-start | bytes 16384 | tf_op jit(solution)/shard_map/all_to_all | solution.py:117
  43.0 0.2 fusion.4
  43.2 0.7 copy.74
  43.9 0.1 copy.92
  44.0 4.6 %all-to-all-done = f32[4,1,4,8]{3,2,1,0:T(4,128)S(1)} async-done(((f32[4,1,4,8]{3,2,1,0:T(4,128)}), f32[4,1,4,8]{3,2,1,0:T(4,128)S(1)}, u32[]{:S(2)}, u32[]{:S(2)}) %all-to-all-start) | async-done | bytes 544 | tf_op jit(solution)/shard_map/all_to_all | solution.py:117
  48.6 3.3 %all-to-all-start.1 = ((f32[1,4,32,128]{3,1,0,2:T(4,128)}), f32[1,4,32,128]{3,1,0,2:T(4,128)S(1)}, u32[]{:S(2)}, u32[]{:S(2)}) async-start(f32[1,4,32,128]{3,1,0,2:T(4,128)} %copy.74), calls=%async_computation.1 | async-start | bytes 131072 | tf_op jit(solution)/shard_map/all_to_all | solution.py:128
  51.9 0.0 all-reduce.3.cloned.1.call-start
  52.0 5.6 %all-to-all-done.1 = f32[1,4,32,128]{3,1,0,2:T(4,128)S(1)} async-done(((f32[1,4,32,128]{3,1,0,2:T(4,128)}), f32[1,4,32,128]{3,1,0,2:T(4,128)S(1)}, u32[]{:S(2)}, u32[]{:S(2)}) %all-to-all-start.1) | async-done | bytes 65568 | tf_op jit(solution)/shard_map/all_to_all | solution.py:128
  57.6 0.1 fusion.11
  57.6 0.1 fusion.29
  57.7 8.7 %fusion.22 = f32[4,8192]{1,0:T(4,128)} fusion(bf16[1024,8192]{1,0:T(8,128)(2,1)} %param.22, bf16[1,4,8,128]{3,2,1,0:T(8,128)(2,1)S(1)} %fusion.29), kind=kOutput, calls=%fused_computation.30 | convolution fusion | flops 67108864 | bytes 16916480 | tf_op jit(solution)/shard_map/dot_general | solution.py:141
  66.4 0.0 all-reduce.3.cloned.1.call-update
  66.5 0.0 copy-done.2
  66.5 0.0 copy-done.3
  66.5 0.6 dynamic-slice.4
  67.1 32.7 %all-reduce.3.cloned.1.call-done = f32[4,8192]{1,0:T(4,128)} async-done(((f32[4,8192]{1,0:T(4,128)}), f32[4,8192]{1,0:T(4,128)}) %all-reduce.3.cloned.1.call-update) | async-done | bytes 131088
  99.8 0.0 copy-done.1
  99.8 2.2 %multiply_reduce_fusion = (f32[]{:T(128)}, f32[1,8192]{1,0:T(1,128)S(1)}) fusion(f32[4,8192]{1,0:T(4,128)} %all-reduce.3.cloned.1.call-done, u32[]{:T(128)} %bitcast.34, bf16[1,8192]{1,0:T(2,128)(2,1)S(1)} %copy-done.1), kind=kLoop, calls=%fused_computation.22 | loop fusion | flops 32767 | bytes 81928 | tf_op jit(solution)/shard_map/reduce_sum | solution.py:148
  102.7 0.7 multiply_convert_fusion
  (15 shorter events, 0.2 us)
Async XLA Ops:
  7.2 20.2 %copy-start = (bf16[1,1024]{1,0:T(2,128)(2,1)S(1)}, bf16[1,1024]{1,0:T(2,128)(2,1)}, u32[]{:S(2)}) copy-start(bf16[1,1024]{1,0:T(2,128)(2,1)} %param.13) | copy-start | bytes 6148
  7.2 59.3 %copy-start.3 = (u32[32]{0:T(128)S(1)}, u32[32]{0:T(128)}, u32[]{:S(2)}) copy-start(u32[32]{0:T(128)} %constant.37) | copy-start | bytes 388
  7.2 59.3 %copy-start.2 = (bf16[8192]{0:T(1024)(128)(2,1)S(1)}, bf16[8192]{0:T(1024)(128)(2,1)}, u32[]{:S(2)}) copy-start(bf16[8192]{0:T(1024)(128)(2,1)} %param.23) | copy-start | bytes 49156
  7.2 92.6 %copy-start.1 = (bf16[1,8192]{1,0:T(2,128)(2,1)S(1)}, bf16[1,8192]{1,0:T(2,128)(2,1)}, u32[]{:S(2)}) copy-start(bf16[1,8192]{1,0:T(2,128)(2,1)} %param.21) | copy-start | bytes 49156
  29.3 10.3 %all-to-all-start.2 = ((f32[1,4,32]{1,0,2:T(1,128)}), f32[1,4,32]{1,0,2:T(1,128)S(1)}, u32[]{:S(2)}, u32[]{:S(2)}) async-start(f32[1,4,32]{1,0,2:T(1,128)} %bitcast.26), calls=%async_computation.2 | async-start | bytes 32768 | tf_op jit(solution)/shard_map/all_to_all | solution.py:127
  39.7 8.9 %all-to-all-start = ((f32[4,1,4,8]{3,2,1,0:T(4,128)}), f32[4,1,4,8]{3,2,1,0:T(4,128)S(1)}, u32[]{:S(2)}, u32[]{:S(2)}) async-start(f32[4,1,4,8]{3,2,1,0:T(4,128)} %pad_maximum_fusion), calls=%async_computation | async-start | bytes 16384 | tf_op jit(solution)/shard_map/all_to_all | solution.py:117
  48.6 9.0 %all-to-all-start.1 = ((f32[1,4,32,128]{3,1,0,2:T(4,128)}), f32[1,4,32,128]{3,1,0,2:T(4,128)S(1)}, u32[]{:S(2)}, u32[]{:S(2)}) async-start(f32[1,4,32,128]{3,1,0,2:T(4,128)} %copy.74), calls=%async_computation.1 | async-start | bytes 131072 | tf_op jit(solution)/shard_map/all_to_all | solution.py:128
  51.9 48.0 %all-reduce.3.cloned.1.call-start = ((), (), s32[]{:S(2)}) async-start(), calls=%async_computation.3 | async-start | bytes 262144
Sparse Core Ops, SparseCore 0:
  66.6 33.1 all-reduce.2
